TPU v7x, 256 devices: a whole 4x4x8 slice. The times are simulated.
256 devices in a mesh: row: 32 (over y, z_lo, core), col: 8 (over z_hi, x).
Axes of the slice: x: 4, y: 4, z: 8 (z_hi: 2, z_lo: 4; z = z_hi * 4 + z_lo), core: 2. Of those that a mesh axis runs over, the one named last changes fastest.
Arguments:
- left: bfloat16 [16384, 16384], P('row', 'col'), may hold values from -6 to 6
- right: bfloat16 [16384, 16384], P('row', 'col'), may hold values from -0.125 to 0.125
Outputs:
- product: bfloat16 [16384, 16384], P('row', 'col')
All inputs are finite; a program needn't handle non-finite values.
Results may differ from a plain program's by a relative error of at most 0.001.
Values may be sent and summed in bfloat16 or wider, within the bound.
A program may use at most 64 MiB of HBM per device.

v0:
```python
import jax
import jax.numpy as jnp
from jax import lax
from jax.sharding import PartitionSpec as P

STEPS = 4


def broadcast(value, axis, source):
    kept = jnp.where(lax.axis_index(axis) == source, value, 0).astype(value.dtype)
    return lax.psum(kept, axis)


def from_behind(block, axis, distance):
    devices = range(lax.axis_size(axis))
    route = [((i - distance) % len(devices), i) for i in devices]
    return lax.ppermute(block, axis, route)


def local(left, right):
    grid_rows = lax.axis_size("row")
    col_count = lax.axis_size("col")
    block_rows = left.shape[0]
    per_shard = grid_rows // col_count
    row_index = lax.axis_index("row")
    partial_sum = jnp.zeros((block_rows, right.shape[1]), jnp.float32)
    right_rows = right
    for offset in range(STEPS):
        kblock = (row_index + offset) % grid_rows
        left_piece = lax.dynamic_slice_in_dim(left, kblock % per_shard * block_rows, block_rows, 1)
        left_block = broadcast(left_piece, "col", kblock // per_shard)
        if offset > 0:
            right_rows = from_behind(right_rows, "row", -1)
        partial_sum = partial_sum + jnp.dot(
            left_block, right_rows, preferred_element_type=jnp.float32
        )
    return partial_sum.astype(jnp.bfloat16)


def solution(mesh):
    return jax.shard_map(
        local,
        mesh=mesh,
        in_specs=(P("row", "col"), P("row", "col")),
        out_specs=P("row", "col"),
        check_vma=False,
    )
```

profile of v0, /device:TPU:6, one launch (start us, length us, event | category | flops | bytes accessed | tf_op | source)
XLA Modules:
  0.0 230.2 jit_solution(6569015499091288478)
XLA Ops:
  6.5 0.0 all-reduce.3.cloned.1.call-start
  6.5 6.5 %collective-permute-start = (bf16[512,2048]{1,0:T(8,128)(2,1)}, bf16[512,2048]{1,0:T(8,128)(2,1)S(1)}, u32[]{:S(2)}, u32[]{:S(2)}) collective-permute-start(bf16[512,2048]{1,0:T(8,128)(2,1)} %param.3), channel_id=1, source_target_pairs={{8,0},{16,8},{24,16},{32,24},{40,32},{48,40},{56,48},{64,56},{72,6... | collective-permute-start | bytes 6291464 | tf_op jit(solution)/shard_map/ppermute | solution.py:17
  13.1 23.9 %collective-permute-done = bf16[512,2048]{1,0:T(8,128)(2,1)S(1)} collective-permute-done((bf16[512,2048]{1,0:T(8,128)(2,1)}, bf16[512,2048]{1,0:T(8,128)(2,1)S(1)}, u32[]{:S(2)}, u32[]{:S(2)}) %collective-permute-start) | collective-permute-done | bytes 2097184 | tf_op jit(solution)/shard_map/ppermute | solution.py:17
  36.9 0.0 copy-start
  36.9 5.7 %collective-permute-start.1 = (bf16[512,2048]{1,0:T(8,128)(2,1)S(1)}, bf16[512,2048]{1,0:T(8,128)(2,1)}, u32[]{:S(2)}, u32[]{:S(2)}) collective-permute-start(bf16[512,2048]{1,0:T(8,128)(2,1)S(1)} %collective-permute-done), channel_id=1, source_target_pairs={{8,0},{16,8},{24,16},{32,24},{40,32},{48,40},{56,48},{64,56},{72,6... | collective-permute-start | bytes 6291464 | tf_op jit(solution)/shard_map/ppermute | solution.py:17
  42.6 3.1 %dynamic-slice_select_fusion = (bf16[512,512]{1,0:T(8,128)(2,1)}, bf16[512,512]{1,0:T(8,128)(2,1)}, bf16[512,512]{1,0:T(8,128)(2,1)}, bf16[512,512]{1,0:T(8,128)(2,1)}) fusion(bf16[512,2048]{1,0:T(8,128)(2,1)} %param.2, s32[]{:T(128)S(6)} %select_n.108, pred[]{:T(512)S(6)} %eq.24, s32[]{:T(128)S(6)} %select_n.96, pred[]{:T(512)S(6)} %eq.22, s32[]{:T(128)S(6)} %select_n.90, ...), kind=kLoop, calls=%fused_computation.1 | loop fusion | flops 1048576 | bytes 4194324 | tf_op jit(solution)/shard_map/jit(_where)/select_n | solution.py:10
  45.7 0.0 copy-done
  45.7 0.0 all-reduce.3.cloned.1.call-update
  45.7 29.5 %collective-permute-done.1 = bf16[512,2048]{1,0:T(8,128)(2,1)} collective-permute-done((bf16[512,2048]{1,0:T(8,128)(2,1)S(1)}, bf16[512,2048]{1,0:T(8,128)(2,1)}, u32[]{:S(2)}, u32[]{:S(2)}) %collective-permute-start.1) | collective-permute-done | bytes 2097184 | tf_op jit(solution)/shard_map/ppermute | solution.py:17
  75.2 6.2 %collective-permute-start.2 = (bf16[512,2048]{1,0:T(8,128)(2,1)}, bf16[512,2048]{1,0:T(8,128)(2,1)S(1)}, u32[]{:S(2)}, u32[]{:S(2)}) collective-permute-start(bf16[512,2048]{1,0:T(8,128)(2,1)} %collective-permute-done.1), channel_id=1, source_target_pairs={{8,0},{16,8},{24,16},{32,24},{40,32},{48,40},{56,48},{64,56},{72,6... | collective-permute-start | bytes 6291464 | tf_op jit(solution)/shard_map/ppermute | solution.py:17
  81.4 131.7 %all-reduce.3.cloned.1.call-done = (bf16[512,512]{1,0:T(8,128)(2,1)}, bf16[512,512]{1,0:T(8,128)(2,1)}, bf16[512,512]{1,0:T(8,128)(2,1)}, bf16[512,512]{1,0:T(8,128)(2,1)}) async-done(((bf16[512,512]{1,0:T(8,128)(2,1)}, bf16[512,512]{1,0:T(8,128)(2,1)}, bf16[512,512]{1,0:T(8,128)(2,1)}, bf16[512,512]{1,0:T(8,128)(2,1)}), (bf16[512,512]{1,0:T(8,128)(2,1)}, bf16[512,512]{1,0:T(8,128)(2,1)}, ...) | async-done | bytes 2097168 | tf_op jit(solution)/shard_map/psum | solution.py:11
  213.2 0.0 copy-start.1
  213.2 0.0 copy-start.4
  213.2 3.2 %fusion = f32[512,2048]{1,0:T(8,128)S(1)} fusion(bf16[512,512]{1,0:T(8,128)(2,1)} %get-tuple-element.6, bf16[512,2048]{1,0:T(8,128)(2,1)} %param.3), kind=kOutput, calls=%fused_computation.5 | convolution fusion | flops 1073741824 | bytes 6815744 | tf_op jit(solution)/shard_map/dot_general | solution.py:34
  216.3 0.0 copy-done.1
  216.3 0.0 copy-done.4
  216.3 0.0 copy-start.3
  216.3 1.3 fusion.1
  217.6 0.0 copy-done.3
  217.6 0.0 copy-start.2
  217.6 2.9 %fusion.2 = f32[512,2048]{1,0:T(8,128)S(1)} fusion(bf16[512,512]{1,0:T(8,128)(2,1)S(1)} %copy-done.3, bf16[512,2048]{1,0:T(8,128)(2,1)} %collective-permute-done.1), kind=kOutput, calls=%fused_computation.7 | convolution fusion | flops 1073741824 | bytes 6815744 | tf_op jit(solution)/shard_map/dot_general | solution.py:34
  220.6 0.0 collective-permute-done.2
  220.6 0.0 copy-done.2
  220.6 2.8 %add_convert_fusion = bf16[512,2048]{1,0:T(8,128)(2,1)} fusion(f32[512,2048]{1,0:T(8,128)S(1)} %fusion.2, f32[512,2048]{1,0:T(8,128)S(1)} %fusion, f32[512,2048]{1,0:T(8,128)S(1)} %fusion.1, bf16[512,512]{1,0:T(8,128)(2,1)S(1)} %copy-done.2, bf16[512,2048]{1,0:T(8,128)(2,1)S(1)} %collective-permute-done.2), kind=kOutput, calls=%fused_computation | convolution fusion | flops 1077936128 | bytes 17301504 | tf_op jit(solution)/shard_map/dot_general | solution.py:34
Async XLA Ops:
  6.5 206.6 %all-reduce.3.cloned.1.call-start = ((), (), s32[]{:S(2)}) async-start(), calls=%async_computation | async-start | bytes 4194304 | tf_op jit(solution)/shard_map/psum | solution.py:11
  6.5 30.4 %collective-permute-start = (bf16[512,2048]{1,0:T(8,128)(2,1)}, bf16[512,2048]{1,0:T(8,128)(2,1)S(1)}, u32[]{:S(2)}, u32[]{:S(2)}) collective-permute-start(bf16[512,2048]{1,0:T(8,128)(2,1)} %param.3), channel_id=1, source_target_pairs={{8,0},{16,8},{24,16},{32,24},{40,32},{48,40},{56,48},{64,56},{72,6... | collective-permute-start | bytes 6291464 | tf_op jit(solution)/shard_map/ppermute | solution.py:17
  36.9 8.8 %copy-start = (bf16[512,2048]{1,0:T(8,128)(2,1)}, bf16[512,2048]{1,0:T(8,128)(2,1)S(1)}, u32[]{:S(2)}) copy-start(bf16[512,2048]{1,0:T(8,128)(2,1)S(1)} %collective-permute-done) | copy-start | bytes 6291460
  36.9 38.3 %collective-permute-start.1 = (bf16[512,2048]{1,0:T(8,128)(2,1)S(1)}, bf16[512,2048]{1,0:T(8,128)(2,1)}, u32[]{:S(2)}, u32[]{:S(2)}) collective-permute-start(bf16[512,2048]{1,0:T(8,128)(2,1)S(1)} %collective-permute-done), channel_id=1, source_target_pairs={{8,0},{16,8},{24,16},{32,24},{40,32},{48,40},{56,48},{64,56},{72,6... | collective-permute-start | bytes 6291464 | tf_op jit(solution)/shard_map/ppermute | solution.py:17
  75.2 145.4 %collective-permute-start.2 = (bf16[512,2048]{1,0:T(8,128)(2,1)}, bf16[512,2048]{1,0:T(8,128)(2,1)S(1)}, u32[]{:S(2)}, u32[]{:S(2)}) collective-permute-start(bf16[512,2048]{1,0:T(8,128)(2,1)} %collective-permute-done.1), channel_id=1, source_target_pairs={{8,0},{16,8},{24,16},{32,24},{40,32},{48,40},{56,48},{64,56},{72,6... | collective-permute-start | bytes 6291464 | tf_op jit(solution)/shard_map/ppermute | solution.py:17
  213.2 3.2 %copy-start.1 = (bf16[512,2048]{1,0:T(8,128)(2,1)S(1)}, bf16[512,2048]{1,0:T(8,128)(2,1)}, u32[]{:S(2)}) copy-start(bf16[512,2048]{1,0:T(8,128)(2,1)} %copy-done) | copy-start | bytes 6291460
  213.2 3.2 %copy-start.4 = (bf16[512,512]{1,0:T(8,128)(2,1)S(1)}, bf16[512,512]{1,0:T(8,128)(2,1)}, u32[]{:S(2)}) copy-start(bf16[512,512]{1,0:T(8,128)(2,1)} %get-tuple-element.7) | copy-start | bytes 1572868
  216.3 1.3 copy-start.3
  217.6 3.0 %copy-start.2 = (bf16[512,512]{1,0:T(8,128)(2,1)S(1)}, bf16[512,512]{1,0:T(8,128)(2,1)}, u32[]{:S(2)}) copy-start(bf16[512,512]{1,0:T(8,128)(2,1)} %get-tuple-element.8) | copy-start | bytes 1572868
Sparse Core Ops, SparseCore 0:
  45.8 167.2 all-reduce.2
where the time goes:
time: 230 us
  waiting for transfers between devices  185 us (80%)
  starting transfers between devices  18.4 us (8%)
  between operations  13.5 us (6%)
  matrix products  10.2 us (4%)
  other arithmetic  3.06 us (1%)
    psum x1, waiting for transfers between devices, broadcast(): return lax.psum(kept, axis)  132 us
    ppermute x3, waiting for transfers between devices, from_behind(): return lax.ppermute(block, axis, route)  53.3 us
    ppermute x3, starting transfers between devices, from_behind(): return lax.ppermute(block, axis, route)  18.4 us
    dot_general x4, matrix products, local(): jnp.dot(left_block, right_rows, preferred_element_type=jnp.float32)  10.2 us
  transfers between devices with their start and end apart: 4, of which 3 were waited for; matrix products, arithmetic and copies ran while one was open for 5% of the time, Pallas kernels for 0%

commit v1 on v0

v1 whole, which is shorter than its diff:
```python
import jax
import jax.numpy as jnp
from jax import lax
from jax.experimental import pallas as pl
from jax.experimental.pallas import tpu as pltpu
from jax.sharding import PartitionSpec as P

MESH = pl.DeviceIdType.MESH
STEPS = 4
CHUNKS = 8
AHEAD = 3
QUARTERS = 4
TOWARDS = (1, 1, -1, -1)
CROSSES = (1, 2, 1, 0)
NEAR = [(s, t) for ts in ((2, 1), (3, 0)) for s in range(STEPS) for t in ts]
FAR = [(s, 3) for s in range(STEPS)] + [(s, t) for s in range(STEPS) for t in (2, 1)] + [(s, 0) for s in range(STEPS)]


def remote(src, dst, sent, got, device):
    return pltpu.make_async_remote_copy(
        src_ref=src, dst_ref=dst, send_sem=sent, recv_sem=got, device_id=device, device_id_type=MESH
    )


def kernel(
    left, right, out, fetched, own, blocks, total, result,
    own_sent, pass_sent, next_sent, next_pass_sent, got, x_sent, cross_sent, piece_got, local, stored,
):
    r, c = lax.axis_index("row"), lax.axis_index("col")
    rows, cols = lax.axis_size("row"), lax.axis_size("col")
    core, q, chips = lax.rem(r, 2), lax.div(r, 2), rows // 2
    ring = cols // 2
    half, x = lax.div(c, ring), lax.rem(c, ring)
    size, width = blocks.shape[1], right.shape[1] // CHUNKS
    tall = size // QUARTERS

    def chip(distance, which):
        return {"row": lax.rem(q + distance + chips, chips) * 2 + which}

    def along(distance):
        return {"col": half * ring + lax.rem(x + distance + ring, ring)}

    across = {"col": (1 - half) * ring + x}
    partner = {"row": q * 2 + 1 - core}

    def columns(i):
        return pl.ds(i * width, width)

    owner, offset = [], []
    for s in range(STEPS):
        owner.append(lax.rem(lax.div(r + s, STEPS), cols))
        offset.append(lax.rem(r + s, STEPS) * size)

    def load_left(s):
        at = pl.ds(pl.multiple_of(offset[s], size), size)
        return pltpu.make_async_copy(left.at[:, at], blocks.at[s], local.at[s])

    load_own = pltpu.make_async_copy(right, own, local.at[STEPS])
    load_own.start()
    for s in range(STEPS):
        @pl.when(c == owner[s])
        def _(s=s):
            load_left(s).start()

    barrier = pltpu.get_barrier_semaphore()
    met = [chip(1, 0), chip(1, 1), chip(-1, 0), chip(-1, 1), partner, along(1), along(-1), across]
    for device in met:
        pl.semaphore_signal(barrier, inc=1, device_id=device, device_id_type=MESH)
    pl.semaphore_wait(barrier, len(met))

    def send_own(i):
        return remote(own.at[:, columns(i)], fetched.at[1, :, columns(i)], own_sent.at[i], got.at[1, i], chip(-1, core))

    def own_to_partner(i):
        return remote(own.at[:, columns(i)], fetched.at[0, :, columns(i)], next_sent.at[i], got.at[0, i], partner)

    def pass_down(i):
        return remote(fetched.at[1, :, columns(i)], fetched.at[2, :, columns(i)], pass_sent.at[i], got.at[2, i], chip(-1, 1))

    def to_partner(i, slot):
        return remote(
            fetched.at[1, :, columns(i)], fetched.at[slot, :, columns(i)], next_pass_sent.at[i], got.at[slot, i], partner
        )

    def place(s, t):
        shift = lax.rem(x - lax.rem(owner[s], ring) + ring, ring)
        hops = shift if TOWARDS[t] > 0 else lax.rem(ring - shift, ring)
        near = half == lax.div(owner[s], ring)
        entered = jnp.where(near, hops, lax.rem(hops - CROSSES[t] + ring, ring))
        return near, hops, entered

    def piece(s, t):
        return blocks.at[s, pl.ds(t * tall, tall), :]

    def send_x(s, t):
        return remote(piece(s, t), piece(s, t), x_sent.at[s, t], piece_got.at[s, t], along(TOWARDS[t]))

    def send_across(s, t):
        return remote(piece(s, t), piece(s, t), cross_sent.at[s, t], piece_got.at[s, t], across)

    def hand_on(s, t, near, hops, entered):
        @pl.when(near & (hops == CROSSES[t]))
        def _():
            send_across(s, t).start()

        @pl.when(entered < ring - 1)
        def _():
            send_x(s, t).start()

    def take(s, t, wanted_near):
        near, hops, entered = place(s, t)

        @pl.when((near == wanted_near) & (jnp.logical_not(near) | (hops > 0)))
        def _():
            send_x(s, t).wait_recv()
            hand_on(s, t, near, hops, entered)

    load_own.wait()
    for i in range(AHEAD):
        send_own(i).start()
    for s in range(STEPS):
        @pl.when(c == owner[s])
        def _(s=s):
            load_left(s).wait()
    for s, t in NEAR:
        near, hops, entered = place(s, t)

        @pl.when(near & (hops == 0))
        def _(s=s, t=t, near=near, hops=hops, entered=entered):
            hand_on(s, t, near, hops, entered)

    @pl.when(core == 1)
    def _():
        for i in range(CHUNKS):
            own_to_partner(i).start()

    per_near, per_far = 4, 2
    for i in range(CHUNKS):
        send_own(i).wait_recv()
        if i + AHEAD < CHUNKS:
            send_own(i + AHEAD).start()

        @pl.when(core == 0)
        def _(i=i):
            to_partner(i, 0).start()
            if i + AHEAD >= CHUNKS:
                pass_down(i + AHEAD - CHUNKS).start()

        @pl.when(core == 1)
        def _(i=i):
            to_partner(i, 2).start()
        for s, t in NEAR[i * per_near : (i + 1) * per_near]:
            take(s, t, True)
        for s, t in FAR[i * per_far : (i + 1) * per_far]:
            take(s, t, False)

    @pl.when(core == 0)
    def _():
        for i in range(AHEAD, CHUNKS):
            pass_down(i).start()

    def dot(s, value):
        return jnp.dot(blocks[s], value, preferred_element_type=jnp.float32)

    @pl.loop(0, CHUNKS)
    def _(i):
        at = pl.ds(pl.multiple_of(i * width, width), width)
        remote(own.at[:, at], fetched.at[0, :, at], own_sent.at[i], got.at[0, i], partner).wait_recv()
        total[:, at] = dot(0, own[:, at]) + dot(1, fetched[0, :, at]) + dot(2, fetched[1, :, at])

    @pl.loop(0, CHUNKS)
    def _(i):
        at = pl.ds(pl.multiple_of(i * width, width), width)
        remote(own.at[:, at], fetched.at[2, :, at], own_sent.at[i], got.at[2, i], partner).wait_recv()
        result[:, at] = (total[:, at] + dot(3, fetched[2, :, at])).astype(result.dtype)
        pltpu.make_async_copy(result.at[:, at], out.at[:, at], stored.at[i]).start()

    for i in range(CHUNKS):
        send_own(i).wait_send()
        to_partner(i, 0).wait_send()

        @pl.when(core == 0)
        def _(i=i):
            pass_down(i).wait_send()

        @pl.when(core == 1)
        def _(i=i):
            own_to_partner(i).wait_send()
    for s in range(STEPS):
        for t in range(QUARTERS):
            near, hops, entered = place(s, t)

            @pl.when(near & (hops == CROSSES[t]))
            def _(s=s, t=t):
                send_across(s, t).wait_send()

            @pl.when(entered < ring - 1)
            def _(s=s, t=t):
                send_x(s, t).wait_send()
    for i in range(CHUNKS):
        pltpu.make_async_copy(result.at[:, columns(i)], out.at[:, columns(i)], stored.at[i]).wait()


def local(left, right):
    size, width = right.shape
    dma = pltpu.SemaphoreType.DMA
    return pl.pallas_call(
        kernel,
        out_shape=jax.ShapeDtypeStruct((size, width), jnp.bfloat16),
        in_specs=[pl.BlockSpec(memory_space=pl.ANY)] * 2,
        out_specs=pl.BlockSpec(memory_space=pl.ANY),
        scratch_shapes=[
            pltpu.VMEM((STEPS - 1, size, width), jnp.bfloat16),
            pltpu.VMEM((size, width), jnp.bfloat16),
            pltpu.VMEM((STEPS, size, size), jnp.bfloat16),
            pltpu.VMEM((size, width), jnp.float32),
            pltpu.VMEM((size, width), jnp.bfloat16),
            dma((CHUNKS,)), dma((CHUNKS,)), dma((CHUNKS,)), dma((CHUNKS,)), dma((STEPS - 1, CHUNKS)),
            dma((STEPS, QUARTERS)), dma((STEPS, QUARTERS)), dma((STEPS, QUARTERS)), dma((STEPS + 1,)), dma((CHUNKS,)),
        ],
        compiler_params=pltpu.CompilerParams(collective_id=0, has_side_effects=True, vmem_limit_bytes=56 * 2**20),
    )(left, right)


def solution(mesh):
    return jax.shard_map(
        local,
        mesh=mesh,
        in_specs=(P("row", "col"), P("row", "col")),
        out_specs=P("row", "col"),
        check_vma=False,
    )
```

time: 230 us -> 203 us (0.88)
  the two profiles are of different devices: /device:TPU:6 before, /device:TPU:51 now
where the time goes in v1:
time: 203 us
  Pallas kernels  200 us (99%)
  local copies, waits for them, and re-layouts  3.16 us (2%)
    pallas_call x1, Pallas kernels, local(): pl.pallas_call(kernel, out_shape=jax.ShapeDtypeStruct((size, width), jnp....  200 us

profile of v1, /device:TPU:51, one launch (start us, length us, event | category | flops | bytes accessed | tf_op | source)
XLA Modules:
  0.0 202.8 jit_solution(10999553973932996500)
XLA Ops:
  0.0 199.6 %shard_map.28 = bf16[512,2048]{1,0:T(8,128)(2,1)} custom-call(bf16[512,2048]{1,0:T(8,128)(2,1)} %left.1, bf16[512,2048]{1,0:T(8,128)(2,1)} %right.1), custom_call_target="tpu_custom_call" | custom-call | tf_op jit(solution)/shard_map/pallas_call | solution.py:207
  199.6 3.2 %copy.4 = bf16[512,2048]{1,0:T(8,128)(2,1)} copy(bf16[512,2048]{1,0:T(8,128)(2,1)} %shard_map.28) | data formatting | bytes 4194304

commit v2 on v1

v2 whole, which is shorter than its diff:
```python
import jax
import jax.numpy as jnp
from jax import lax
from jax.experimental import pallas as pl
from jax.experimental.pallas import tpu as pltpu
from jax.sharding import PartitionSpec as P

MESH = pl.DeviceIdType.MESH
STEPS = 4
RUN = 4
CHUNKS = 8
AHEAD = 4
QUARTERS = 4
NEAR = (0, 1, 2, 3)
FAR = (3, 4, 5, 6)
RELAY = (2, 3, 4, 5)


def remote(src, dst, sent, got, device):
    return pltpu.make_async_remote_copy(
        src_ref=src, dst_ref=dst, send_sem=sent, recv_sem=got, device_id=device, device_id_type=MESH
    )


def kernel(
    left, right, out, fetched, own, blocks, total, result,
    own_sent, pass_sent, next_sent, next_pass_sent, got, x_sent, scatter_sent, cross_sent, piece_got, local, stored,
    transit, transit_got, relay_sent, closing_sent,
):
    r, c = lax.axis_index("row"), lax.axis_index("col")
    rows, cols = lax.axis_size("row"), lax.axis_size("col")
    core, q, chips = lax.rem(r, 2), lax.div(r, 2), rows // 2
    ring = cols // 2
    half, x = lax.div(c, ring), lax.rem(c, ring)
    size, width = blocks.shape[1], right.shape[1] // CHUNKS
    tall = size // QUARTERS

    def chip(distance, which):
        return {"row": lax.rem(q + distance + chips, chips) * 2 + which}

    def along(distance):
        return {"col": half * ring + lax.rem(x + distance + ring, ring)}

    across = {"col": (1 - half) * ring + x}
    along_z = lax.rem(q, RUN)
    ends = jnp.logical_or(along_z == 0, along_z == RUN - 1)
    relayed = jnp.logical_and(ends, core == 1)
    other_end = jnp.where(along_z == 0, r + 2 * (RUN - 1), jnp.where(along_z == RUN - 1, r - 2 * (RUN - 1), r))
    partner = {"row": q * 2 + 1 - core}

    def columns(i):
        return pl.ds(i * width, width)

    owner, offset = [], []
    for s in range(STEPS):
        owner.append(lax.rem(lax.div(r + s, STEPS), cols))
        offset.append(lax.rem(r + s, STEPS) * size)

    def load_left(s):
        at = pl.ds(pl.multiple_of(offset[s], size), size)
        return pltpu.make_async_copy(left.at[:, at], blocks.at[s], local.at[s])

    load_own = pltpu.make_async_copy(right, own, local.at[STEPS])
    load_own.start()
    for s in range(STEPS):
        @pl.when(c == owner[s])
        def _(s=s):
            load_left(s).start()

    barrier = pltpu.get_barrier_semaphore()
    met = [partner, along(1), along(2), along(3), across]
    first, last = along_z == 0, along_z == RUN - 1
    leaps_down = jnp.logical_and(along_z <= 1, core == 0)
    leaps_up = jnp.logical_and(along_z >= RUN - 2, core == 1)
    groups = [
        (jnp.logical_not(first), [chip(-1, 0), chip(-1, 1)]),
        (jnp.logical_not(last), [chip(1, 0), chip(1, 1)]),
        (leaps_down, [chip(-2, 1)]),
        (leaps_up, [chip(2, 0)]),
        (jnp.logical_and(first, core == 1), [chip(-1, 1)]),
        (jnp.logical_and(last, core == 1), [chip(1, 1)]),
        (relayed, [{"row": other_end}, {"row": other_end, **across}]),
    ]
    expected = len(met)
    for needed, devices in groups:
        expected = expected + jnp.where(needed, len(devices), 0)

        @pl.when(needed)
        def _(devices=devices):
            for device in devices:
                pl.semaphore_signal(barrier, inc=1, device_id=device, device_id_type=MESH)
    for device in met:
        pl.semaphore_signal(barrier, inc=1, device_id=device, device_id_type=MESH)
    pl.semaphore_wait(barrier, expected)

    relays_right = jnp.logical_and(along_z == RUN - 2, core == 1)
    skips = jnp.logical_and(first, core == 0)
    below = {"row": jnp.where(skips, chip(-2, 1)["row"], chip(-1, core)["row"])}
    below_slot = jnp.where(skips, 2, 1)

    def send_own(i):
        return remote(
            own.at[:, columns(i)], fetched.at[below_slot, :, columns(i)], own_sent.at[i], got.at[below_slot, i], below
        )

    def next_two(i):
        return remote(own.at[:, columns(i)], fetched.at[1, :, columns(i)], own_sent.at[i], got.at[1, i], partner)

    def closing(i):
        return remote(
            fetched.at[2, :, columns(i)], fetched.at[1, :, columns(i)], closing_sent.at[i], got.at[1, i], chip(1, 0)
        )

    def closing_in(i):
        return remote(own.at[:, columns(i)], fetched.at[2, :, columns(i)], own_sent.at[i], got.at[2, i], partner)

    def leap(i):
        return remote(own.at[:, columns(i)], fetched.at[2, :, columns(i)], closing_sent.at[i], got.at[2, i], chip(-2, 1))

    leaps = jnp.logical_and(along_z == 1, core == 0)
    passes = jnp.logical_and(jnp.logical_or(along_z == 1, along_z == 2), core == 0)

    def own_to_partner(i):
        return remote(own.at[:, columns(i)], fetched.at[0, :, columns(i)], next_sent.at[i], got.at[0, i], partner)

    def pass_down(i):
        return remote(fetched.at[1, :, columns(i)], fetched.at[2, :, columns(i)], pass_sent.at[i], got.at[2, i], chip(-1, 1))

    def to_partner(i, slot):
        return remote(
            fetched.at[1, :, columns(i)], fetched.at[slot, :, columns(i)], next_pass_sent.at[i], got.at[slot, i], partner
        )

    def root(s):
        return lax.rem(owner[s], ring), half == lax.div(owner[s], ring)

    def piece(s, t):
        return blocks.at[s, pl.ds(pl.multiple_of(t * tall, tall), tall), :]

    def line(s, t, d, device):
        return remote(piece(s, t), piece(s, t), x_sent.at[s, d], piece_got.at[s, t], device)

    def scatter(s, d):
        return remote(
            piece(s, lax.rem(x + d, ring)), piece(s, lax.rem(x + d, ring)),
            scatter_sent.at[s, d], piece_got.at[s, lax.rem(x + d, ring)], along(d),
        )

    def gather(s, d):
        return line(s, x, d, along(d))

    def send_across(s):
        return remote(piece(s, x), piece(s, x), cross_sent.at[s], piece_got.at[s, x], across)

    def send_to_relay(s):
        return remote(piece(s, x), transit.at[s], cross_sent.at[s], transit_got.at[s], {"row": other_end, **across})

    def relay(s):
        return remote(transit.at[s], piece(s, x), relay_sent.at[s], piece_got.at[s, x], {"row": other_end})

    def relays(s):
        from_half = lax.div(lax.rem(lax.div(other_end + s, STEPS), cols), ring)
        return jnp.logical_and(relayed, half != from_half)

    def hand_on(s):
        @pl.when(relays(s))
        def _():
            send_to_relay(s).wait_recv()
            relay(s).start()

    def wants(s, d):
        at, near = root(s)
        return jnp.logical_not(near & (lax.rem(x + d, ring) == at))

    def is_root(s):
        return c == owner[s]

    def share(s):
        at, near = root(s)

        @pl.when(jnp.logical_and(near, jnp.logical_not(relayed)))
        def _():
            send_across(s).start()

        @pl.when(jnp.logical_and(near, relayed))
        def _():
            send_to_relay(s).start()
        for d in (1, 3, 2):
            @pl.when(wants(s, d))
            def _(d=d):
                gather(s, d).start()

    def take(s, wanted_near):
        at, near = root(s)

        @pl.when((near == wanted_near) & jnp.logical_not(is_root(s)))
        def _():
            gather(s, 1).wait_recv()
            share(s)

    load_own.wait()
    for i in range(AHEAD):
        send_own(i).start()
    for s in range(STEPS):
        @pl.when(c == owner[s])
        def _(s=s):
            load_left(s).wait()
    for s in range(STEPS):
        @pl.when(is_root(s))
        def _(s=s):
            for d in (2, 1, 3):
                scatter(s, d).start()
    for s in range(STEPS):
        @pl.when(is_root(s))
        def _(s=s):
            share(s)

    @pl.when(core == 1)
    def _():
        for i in range(CHUNKS):
            own_to_partner(i).start()

    for i in range(CHUNKS):
        send_own(i).wait_send()
        if i + AHEAD < CHUNKS:
            send_own(i + AHEAD).start()

        @pl.when(jnp.logical_not(last))
        def _(i=i):
            next_two(i).wait_recv()
            to_partner(i, 2 * core).start()

        @pl.when(relays_right)
        def _(i=i):
            closing_in(i).wait_recv()
            closing(i).start()
        if i >= CHUNKS // 2:
            @pl.when(leaps)
            def _(i=i):
                for j in range(2 * i - CHUNKS, 2 * i - CHUNKS + 2):
                    leap(j).start()
        if i + AHEAD >= CHUNKS:
            @pl.when(passes)
            def _(i=i):
                pass_down(i + AHEAD - CHUNKS).start()
        for s in range(STEPS):
            if NEAR[s] == i:
                take(s, True)
            if FAR[s] == i:
                take(s, False)
            if RELAY[s] == i:
                hand_on(s)

    @pl.when(passes)
    def _():
        for i in range(AHEAD, CHUNKS):
            pass_down(i).start()

    def await_left(s):
        @pl.when(jnp.logical_not(is_root(s)))
        def _():
            for d in range(1, ring):
                line(s, lax.rem(x + d, ring), d, along(d)).wait_recv()

    def window(i):
        return pl.ds(pl.multiple_of(i * width, width), width)

    def await_right(slot, i):
        remote(own.at[:, window(i)], fetched.at[slot, :, window(i)], own_sent.at[i], got.at[slot, i], partner).wait_recv()

    def dot(s, value):
        return jnp.dot(blocks[s], value, preferred_element_type=jnp.float32)

    def finish(i, summed):
        result[:, window(i)] = summed.astype(result.dtype)
        pltpu.make_async_copy(result.at[:, window(i)], out.at[:, window(i)], stored.at[i]).start()

    await_left(0)

    @pl.loop(0, CHUNKS)
    def _(i):
        total[:, window(i)] = dot(0, own[:, window(i)])

    @pl.when(jnp.logical_not(last))
    def _():
        for s in range(1, STEPS - 1):
            await_left(s)

            @pl.loop(0, CHUNKS)
            def _(i, s=s):
                if s == 1:
                    await_right(0, i)
                total[:, window(i)] += dot(s, fetched[s - 1, :, window(i)])

        await_left(STEPS - 1)

        @pl.loop(0, CHUNKS)
        def _(i):
            @pl.when(jnp.logical_not(relays_right))
            def _():
                await_right(STEPS - 2, i)
            finish(i, total[:, window(i)] + dot(STEPS - 1, fetched[STEPS - 2, :, window(i)]))

    @pl.when(last)
    def _():
        def forward(i):
            await_right(1, i)
            remote(
                fetched.at[1, :, window(i)], fetched.at[2 * core, :, window(i)],
                next_pass_sent.at[i], got.at[2 * core, i], partner,
            ).start()

        for s in range(1, STEPS):
            await_left(s)
        forward(0)

        @pl.loop(0, CHUNKS)
        def _(i):
            @pl.when(i + 1 < CHUNKS)
            def _():
                forward(i + 1)
            await_right(0, i)
            await_right(2, i)
            summed = total[:, window(i)]
            for s in range(1, STEPS):
                summed += dot(s, fetched[s - 1, :, window(i)])
            finish(i, summed)

    for i in range(CHUNKS):
        to_partner(i, 0).wait_send()

        @pl.when(passes)
        def _(i=i):
            pass_down(i).wait_send()

        @pl.when(jnp.logical_or(relays_right, leaps))
        def _(i=i):
            leap(i).wait_send()

        @pl.when(core == 1)
        def _(i=i):
            own_to_partner(i).wait_send()
    for s in range(STEPS):
        at, near = root(s)

        @pl.when(near)
        def _(s=s):
            send_across(s).wait_send()

        @pl.when(relays(s))
        def _(s=s):
            relay(s).wait_send()
        for d in range(1, ring):
            @pl.when(wants(s, d))
            def _(s=s, d=d):
                gather(s, d).wait_send()

            @pl.when(is_root(s))
            def _(s=s, d=d):
                scatter(s, d).wait_send()
    for i in range(CHUNKS):
        pltpu.make_async_copy(result.at[:, columns(i)], out.at[:, columns(i)], stored.at[i]).wait()


def local(left, right):
    size, width = right.shape
    dma = pltpu.SemaphoreType.DMA
    return pl.pallas_call(
        kernel,
        out_shape=jax.ShapeDtypeStruct((size, width), jnp.bfloat16),
        in_specs=[pl.BlockSpec(memory_space=pl.ANY)] * 2,
        out_specs=pl.BlockSpec(memory_space=pl.ANY),
        scratch_shapes=[
            pltpu.VMEM((STEPS - 1, size, width), jnp.bfloat16),
            pltpu.VMEM((size, width), jnp.bfloat16),
            pltpu.VMEM((STEPS, size, size), jnp.bfloat16),
            pltpu.VMEM((size, width), jnp.float32),
            pltpu.VMEM((size, width), jnp.bfloat16),
            dma((CHUNKS,)), dma((CHUNKS,)), dma((CHUNKS,)), dma((CHUNKS,)), dma((STEPS - 1, CHUNKS)),
            dma((STEPS, QUARTERS)), dma((STEPS, QUARTERS)), dma((STEPS,)), dma((STEPS, QUARTERS)), dma((STEPS + 1,)), dma((CHUNKS,)),
            pltpu.VMEM((STEPS, size // QUARTERS, size), jnp.bfloat16), dma((STEPS,)), dma((STEPS,)), dma((CHUNKS,)),
        ],
        compiler_params=pltpu.CompilerParams(collective_id=0, has_side_effects=True, vmem_limit_bytes=56 * 2**20),
    )(left, right)


def solution(mesh):
    return jax.shard_map(
        local,
        mesh=mesh,
        in_specs=(P("row", "col"), P("row", "col")),
        out_specs=P("row", "col"),
        check_vma=False,
    )
```

time: 203 us -> 106 us (0.52)
  the two profiles are of different devices: /device:TPU:51 before, /device:TPU:107 now
where the time goes in v2:
time: 106 us
  Pallas kernels  103 us (97%)
  local copies, waits for them, and re-layouts  3.16 us (3%)
    pallas_call x1, Pallas kernels, local(): pl.pallas_call(kernel, out_shape=jax.ShapeDtypeStruct((size, width), jnp....  103 us
    unnamed x1, local copies, waits for them, and re-layouts  3.16 us

profile of v2, /device:TPU:107, one launch (start us, length us, event | category | flops | bytes accessed | tf_op | source)
XLA Modules:
  0.0 106.1 jit_solution(3177857081144109359)
XLA Ops:
  0.0 102.9 %shard_map.28 = bf16[512,2048]{1,0:T(8,128)(2,1)} custom-call(bf16[512,2048]{1,0:T(8,128)(2,1)} %left.1, bf16[512,2048]{1,0:T(8,128)(2,1)} %right.1), custom_call_target="tpu_custom_call" | custom-call | tf_op jit(solution)/shard_map/pallas_call | solution.py:368
  103.0 3.2 %copy.4 = bf16[512,2048]{1,0:T(8,128)(2,1)} copy(bf16[512,2048]{1,0:T(8,128)(2,1)} %shard_map.28) | data formatting | bytes 4194304

commit v3 on v2

--- a/solution.py
+++ b/solution.py
@@ -7,8 +7,11 @@
 
 MESH = pl.DeviceIdType.MESH
 STEPS = 4
+FIRST_MORE, LAST_MORE = 2, 0
+EARLY = 2
 RUN = 4
 CHUNKS = 8
+PER = 1
 AHEAD = 4
 QUARTERS = 4
 NEAR = (0, 1, 2, 3)
@@ -23,8 +26,8 @@
 
 
 def kernel(
-    left, right, out, fetched, own, blocks, total, result,
-    own_sent, pass_sent, next_sent, next_pass_sent, got, x_sent, scatter_sent, cross_sent, piece_got, local, stored,
+    left, right, out, fetched, own, blocks, total,
+    own_sent, pass_sent, next_sent, next_pass_sent, got, x_sent, scatter_sent, cross_sent, piece_got, local,
     transit, transit_got, relay_sent, closing_sent,
 ):
     r, c = lax.axis_index("row"), lax.axis_index("col")
@@ -44,7 +47,12 @@
     across = {"col": (1 - half) * ring + x}
     along_z = lax.rem(q, RUN)
     ends = jnp.logical_or(along_z == 0, along_z == RUN - 1)
-    relayed = jnp.logical_and(ends, core == 1)
+
+    def crosses_by_relay(s, at_first):
+        return jnp.logical_or(core == 1, s < jnp.where(at_first, FIRST_MORE, LAST_MORE))
+
+    def relayed(s):
+        return jnp.logical_and(ends, crosses_by_relay(s, along_z == 0))
     other_end = jnp.where(along_z == 0, r + 2 * (RUN - 1), jnp.where(along_z == RUN - 1, r - 2 * (RUN - 1), r))
     partner = {"row": q * 2 + 1 - core}
 
@@ -79,7 +87,7 @@
         (leaps_up, [chip(2, 0)]),
         (jnp.logical_and(first, core == 1), [chip(-1, 1)]),
         (jnp.logical_and(last, core == 1), [chip(1, 1)]),
-        (relayed, [{"row": other_end}, {"row": other_end, **across}]),
+        (ends, [{"row": other_end}, {"row": other_end, **across}]),
     ]
     expected = len(met)
     for needed, devices in groups:
@@ -160,7 +168,7 @@
 
     def relays(s):
         from_half = lax.div(lax.rem(lax.div(other_end + s, STEPS), cols), ring)
-        return jnp.logical_and(relayed, half != from_half)
+        return jnp.logical_and(jnp.logical_and(ends, crosses_by_relay(s, last)), half != from_half)
 
     def hand_on(s):
         @pl.when(relays(s))
@@ -178,11 +186,11 @@
     def share(s):
         at, near = root(s)
 
-        @pl.when(jnp.logical_and(near, jnp.logical_not(relayed)))
+        @pl.when(jnp.logical_and(near, jnp.logical_not(relayed(s))))
         def _():
             send_across(s).start()
 
-        @pl.when(jnp.logical_and(near, relayed))
+        @pl.when(jnp.logical_and(near, relayed(s)))
         def _():
             send_to_relay(s).start()
         for d in (1, 3, 2):
@@ -201,6 +209,11 @@
     load_own.wait()
     for i in range(AHEAD):
         send_own(i).start()
+
+    @pl.when(leaps)
+    def _():
+        for i in range(EARLY):
+            leap(i).start()
     for s in range(STEPS):
         @pl.when(c == owner[s])
         def _(s=s):
@@ -237,18 +250,18 @@
         if i >= CHUNKS // 2:
             @pl.when(leaps)
             def _(i=i):
-                for j in range(2 * i - CHUNKS, 2 * i - CHUNKS + 2):
+                for j in range(max(EARLY, 2 * i - CHUNKS), 2 * i - CHUNKS + 2):
                     leap(j).start()
         if i + AHEAD >= CHUNKS:
             @pl.when(passes)
             def _(i=i):
                 pass_down(i + AHEAD - CHUNKS).start()
         for s in range(STEPS):
-            if NEAR[s] == i:
+            if NEAR[s] * PER + PER - 1 == i:
                 take(s, True)
-            if FAR[s] == i:
+            if FAR[s] * PER + PER - 1 == i:
                 take(s, False)
-            if RELAY[s] == i:
+            if RELAY[s] * PER + PER - 1 == i:
                 hand_on(s)
 
     @pl.when(passes)
@@ -263,21 +276,25 @@
                 line(s, lax.rem(x + d, ring), d, along(d)).wait_recv()
 
     def window(i):
+        return pl.ds(pl.multiple_of(i * (PER * width), PER * width), PER * width)
+
+    def chunk(i):
         return pl.ds(pl.multiple_of(i * width, width), width)
 
     def await_right(slot, i):
-        remote(own.at[:, window(i)], fetched.at[slot, :, window(i)], own_sent.at[i], got.at[slot, i], partner).wait_recv()
+        for j in range(PER):
+            at, n = chunk(i * PER + j), i * PER + j
+            remote(own.at[:, at], fetched.at[slot, :, at], own_sent.at[n], got.at[slot, n], partner).wait_recv()
 
     def dot(s, value):
         return jnp.dot(blocks[s], value, preferred_element_type=jnp.float32)
 
     def finish(i, summed):
-        result[:, window(i)] = summed.astype(result.dtype)
-        pltpu.make_async_copy(result.at[:, window(i)], out.at[:, window(i)], stored.at[i]).start()
+        out[:, window(i)] = summed.astype(out.dtype)
 
     await_left(0)
 
-    @pl.loop(0, CHUNKS)
+    @pl.loop(0, CHUNKS // PER)
     def _(i):
         total[:, window(i)] = dot(0, own[:, window(i)])
 
@@ -286,7 +303,7 @@
         for s in range(1, STEPS - 1):
             await_left(s)
 
-            @pl.loop(0, CHUNKS)
+            @pl.loop(0, CHUNKS // PER)
             def _(i, s=s):
                 if s == 1:
                     await_right(0, i)
@@ -294,7 +311,7 @@
 
         await_left(STEPS - 1)
 
-        @pl.loop(0, CHUNKS)
+        @pl.loop(0, CHUNKS // PER)
         def _(i):
             @pl.when(jnp.logical_not(relays_right))
             def _():
@@ -305,18 +322,19 @@
     def _():
         def forward(i):
             await_right(1, i)
-            remote(
-                fetched.at[1, :, window(i)], fetched.at[2 * core, :, window(i)],
-                next_pass_sent.at[i], got.at[2 * core, i], partner,
-            ).start()
+            for j in range(PER):
+                at, n = chunk(i * PER + j), i * PER + j
+                remote(
+                    fetched.at[1, :, at], fetched.at[2 * core, :, at], next_pass_sent.at[n], got.at[2 * core, n], partner
+                ).start()
 
         for s in range(1, STEPS):
             await_left(s)
         forward(0)
 
-        @pl.loop(0, CHUNKS)
+        @pl.loop(0, CHUNKS // PER)
         def _(i):
-            @pl.when(i + 1 < CHUNKS)
+            @pl.when(i + 1 < CHUNKS // PER)
             def _():
                 forward(i + 1)
             await_right(0, i)
@@ -358,8 +376,6 @@
             @pl.when(is_root(s))
             def _(s=s, d=d):
                 scatter(s, d).wait_send()
-    for i in range(CHUNKS):
-        pltpu.make_async_copy(result.at[:, columns(i)], out.at[:, columns(i)], stored.at[i]).wait()
 
 
 def local(left, right):
@@ -368,20 +384,19 @@
     return pl.pallas_call(
         kernel,
         out_shape=jax.ShapeDtypeStruct((size, width), jnp.bfloat16),
-        in_specs=[pl.BlockSpec(memory_space=pl.ANY)] * 2,
-        out_specs=pl.BlockSpec(memory_space=pl.ANY),
+        in_specs=[pl.BlockSpec(memory_space=pltpu.HBM)] * 2,
+        out_specs=pl.BlockSpec(memory_space=pltpu.VMEM),
         scratch_shapes=[
             pltpu.VMEM((STEPS - 1, size, width), jnp.bfloat16),
             pltpu.VMEM((size, width), jnp.bfloat16),
             pltpu.VMEM((STEPS, size, size), jnp.bfloat16),
             pltpu.VMEM((size, width), jnp.float32),
-            pltpu.VMEM((size, width), jnp.bfloat16),
             dma((CHUNKS,)), dma((CHUNKS,)), dma((CHUNKS,)), dma((CHUNKS,)), dma((STEPS - 1, CHUNKS)),
-            dma((STEPS, QUARTERS)), dma((STEPS, QUARTERS)), dma((STEPS,)), dma((STEPS, QUARTERS)), dma((STEPS + 1,)), dma((CHUNKS,)),
+            dma((STEPS, QUARTERS)), dma((STEPS, QUARTERS)), dma((STEPS,)), dma((STEPS, QUARTERS)), dma((STEPS + 1,)),
             pltpu.VMEM((STEPS, size // QUARTERS, size), jnp.bfloat16), dma((STEPS,)), dma((STEPS,)), dma((CHUNKS,)),
         ],
-        compiler_params=pltpu.CompilerParams(collective_id=0, has_side_effects=True, vmem_limit_bytes=56 * 2**20),
-    )(left, right)
+        compiler_params=pltpu.CompilerParams(collective_id=0, has_side_effects=True, vmem_limit_bytes=20 * 2**20),
+    )(pltpu.with_memory_space_constraint(left, pltpu.HBM), pltpu.with_memory_space_constraint(right, pltpu.HBM))
 
 
 def solution(mesh):

time: 106 us -> 101 us (0.953)
  Pallas kernels: 103 us -> 99.4 us
  local copies, waits for them, and re-layouts: 3.16 us -> 1.32 us
    pallas_call x1, Pallas kernels: 103 us -> 99.4 us  [local(): pl.pallas_call(kernel, out_shape=jax.ShapeDtypeStruct((size, width), jnp....]
    unnamed x1, local copies, waits for them, and re-layouts: 3.16 us -> 1.32 us
where the time goes in v3:
time: 101 us
  Pallas kernels  99.4 us (98%)
  local copies, waits for them, and re-layouts  1.32 us (1%)
    pallas_call x1, Pallas kernels, local(): pl.pallas_call(kernel, out_shape=jax.ShapeDtypeStruct((size, width), jnp....  99.4 us

profile of v3, /device:TPU:107, one launch (start us, length us, event | category | flops | bytes accessed | tf_op | source)
XLA Modules:
  0.0 100.8 jit_solution(3267814187141257758)
XLA Ops:
  0.0 99.4 %shard_map.28 = bf16[512,2048]{1,0:T(8,128)(2,1)S(1)} custom-call(bf16[512,2048]{1,0:T(8,128)(2,1)} %left.1, bf16[512,2048]{1,0:T(8,128)(2,1)} %right.1), custom_call_target="tpu_custom_call" | custom-call | tf_op jit(solution)/shard_map/pallas_call | solution.py:384
  99.4 1.3 %copy.4 = bf16[512,2048]{1,0:T(8,128)(2,1)} copy(bf16[512,2048]{1,0:T(8,128)(2,1)S(1)} %shard_map.28) | data formatting | bytes 4194304

commit v4 on v3

--- a/solution.py
+++ b/solution.py
@@ -7,7 +7,8 @@
 
 MESH = pl.DeviceIdType.MESH
 STEPS = 4
-FIRST_MORE, LAST_MORE = 2, 0
+FIRST_MORE, LAST_MORE = 1, 1
+THIRD = 2
 EARLY = 2
 RUN = 4
 CHUNKS = 8
@@ -15,7 +16,7 @@
 AHEAD = 4
 QUARTERS = 4
 NEAR = (0, 1, 2, 3)
-FAR = (3, 4, 5, 6)
+FAR = (7, 7, 7, 7)
 RELAY = (2, 3, 4, 5)
 
 
@@ -48,12 +49,15 @@
     along_z = lax.rem(q, RUN)
     ends = jnp.logical_or(along_z == 0, along_z == RUN - 1)
 
-    def crosses_by_relay(s, at_first):
-        return jnp.logical_or(core == 1, s < jnp.where(at_first, FIRST_MORE, LAST_MORE))
+    def crosses_by_relay(s, position):
+        at_end = jnp.logical_or(core == 1, s < jnp.where(position == 0, FIRST_MORE, LAST_MORE))
+        at_third = jnp.logical_and(core == 1, s < THIRD)
+        return jnp.where(position == RUN - 2, at_third, jnp.logical_and(position != 1, at_end))
 
     def relayed(s):
-        return jnp.logical_and(ends, crosses_by_relay(s, along_z == 0))
-    other_end = jnp.where(along_z == 0, r + 2 * (RUN - 1), jnp.where(along_z == RUN - 1, r - 2 * (RUN - 1), r))
+        return crosses_by_relay(s, along_z)
+
+    mate = r + 2 * jnp.where(ends, jnp.where(along_z == 0, RUN - 1, 1 - RUN), jnp.where(along_z == 1, 1, -1))
     partner = {"row": q * 2 + 1 - core}
 
     def columns(i):
@@ -87,7 +91,8 @@
         (leaps_up, [chip(2, 0)]),
         (jnp.logical_and(first, core == 1), [chip(-1, 1)]),
         (jnp.logical_and(last, core == 1), [chip(1, 1)]),
-        (ends, [{"row": other_end}, {"row": other_end, **across}]),
+        (ends, [{"row": mate}]),
+        (jnp.logical_or(ends, core == 1), [{"row": mate, **across}]),
     ]
     expected = len(met)
     for needed, devices in groups:
@@ -160,15 +165,20 @@
     def send_across(s):
         return remote(piece(s, x), piece(s, x), cross_sent.at[s], piece_got.at[s, x], across)
 
+    near_mate = {"row": mate, "col": jnp.where(ends, across["col"], c)}
+    far_mate = {"row": mate, "col": jnp.where(ends, c, across["col"])}
+
     def send_to_relay(s):
-        return remote(piece(s, x), transit.at[s], cross_sent.at[s], transit_got.at[s], {"row": other_end, **across})
+        return remote(piece(s, x), transit.at[s], cross_sent.at[s], transit_got.at[s], near_mate)
 
     def relay(s):
-        return remote(transit.at[s], piece(s, x), relay_sent.at[s], piece_got.at[s, x], {"row": other_end})
+        return remote(transit.at[s], piece(s, x), relay_sent.at[s], piece_got.at[s, x], far_mate)
 
     def relays(s):
-        from_half = lax.div(lax.rem(lax.div(other_end + s, STEPS), cols), ring)
-        return jnp.logical_and(jnp.logical_and(ends, crosses_by_relay(s, last)), half != from_half)
+        from_half = lax.div(lax.rem(lax.div(mate + s, STEPS), cols), ring)
+        position = lax.rem(lax.div(mate, 2), RUN)
+        placed = jnp.where(ends, half != from_half, half == from_half)
+        return jnp.logical_and(crosses_by_relay(s, position), placed)
 
     def hand_on(s):
         @pl.when(relays(s))
@@ -252,10 +262,11 @@
             def _(i=i):
                 for j in range(max(EARLY, 2 * i - CHUNKS), 2 * i - CHUNKS + 2):
                     leap(j).start()
-        if i + AHEAD >= CHUNKS:
+        if i >= CHUNKS // 2:
             @pl.when(passes)
             def _(i=i):
-                pass_down(i + AHEAD - CHUNKS).start()
+                for j in range(2 * i - CHUNKS, 2 * i - CHUNKS + 2):
+                    pass_down(j).start()
         for s in range(STEPS):
             if NEAR[s] * PER + PER - 1 == i:
                 take(s, True)
@@ -264,10 +275,6 @@
             if RELAY[s] * PER + PER - 1 == i:
                 hand_on(s)
 
-    @pl.when(passes)
-    def _():
-        for i in range(AHEAD, CHUNKS):
-            pass_down(i).start()
 
     def await_left(s):
         @pl.when(jnp.logical_not(is_root(s)))
@@ -289,6 +296,26 @@
     def dot(s, value):
         return jnp.dot(blocks[s], value, preferred_element_type=jnp.float32)
 
+    def left_is_sent():
+        for s in range(STEPS):
+            at, near = root(s)
+
+            @pl.when(near)
+            def _(s=s):
+                send_across(s).wait_send()
+
+            @pl.when(relays(s))
+            def _(s=s):
+                relay(s).wait_send()
+            for d in range(1, ring):
+                @pl.when(wants(s, d))
+                def _(s=s, d=d):
+                    gather(s, d).wait_send()
+
+                @pl.when(is_root(s))
+                def _(s=s, d=d):
+                    scatter(s, d).wait_send()
+
     def finish(i, summed):
         out[:, window(i)] = summed.astype(out.dtype)
 
@@ -310,6 +337,9 @@
                 total[:, window(i)] += dot(s, fetched[s - 1, :, window(i)])
 
         await_left(STEPS - 1)
+        left_is_sent()
+        for i in range(CHUNKS):
+            to_partner(i, 0).wait_send()
 
         @pl.loop(0, CHUNKS // PER)
         def _(i):
@@ -331,6 +361,7 @@
         for s in range(1, STEPS):
             await_left(s)
         forward(0)
+        left_is_sent()
 
         @pl.loop(0, CHUNKS // PER)
         def _(i):
@@ -345,7 +376,9 @@
             finish(i, summed)
 
     for i in range(CHUNKS):
-        to_partner(i, 0).wait_send()
+        @pl.when(last)
+        def _(i=i):
+            to_partner(i, 0).wait_send()
 
         @pl.when(passes)
         def _(i=i):
@@ -358,24 +391,6 @@
         @pl.when(core == 1)
         def _(i=i):
             own_to_partner(i).wait_send()
-    for s in range(STEPS):
-        at, near = root(s)
-
-        @pl.when(near)
-        def _(s=s):
-            send_across(s).wait_send()
-
-        @pl.when(relays(s))
-        def _(s=s):
-            relay(s).wait_send()
-        for d in range(1, ring):
-            @pl.when(wants(s, d))
-            def _(s=s, d=d):
-                gather(s, d).wait_send()
-
-            @pl.when(is_root(s))
-            def _(s=s, d=d):
-                scatter(s, d).wait_send()
 
 
 def local(left, right):

time: 101 us -> 99.5 us (0.985)
  Pallas kernels: 99.4 us -> 97.7 us
    pallas_call x1, Pallas kernels: 99.4 us -> 97.7 us  [local(): pl.pallas_call(kernel, out_shape=jax.ShapeDtypeStruct((size, width), jnp....]
where the time goes in v4:
time: 99.5 us; the launch traced here: 99.1 us
  Pallas kernels  97.7 us (98%)
  local copies, waits for them, and re-layouts  1.32 us (1%)
    pallas_call x1, Pallas kernels, local(): pl.pallas_call(kernel, out_shape=jax.ShapeDtypeStruct((size, width), jnp....  97.7 us

profile of v4, /device:TPU:107, one launch (start us, length us, event | category | flops | bytes accessed | tf_op | source)
XLA Modules:
  0.0 99.1 jit_solution(5432881394735928464)
XLA Ops:
  0.0 97.7 %shard_map.28 = bf16[512,2048]{1,0:T(8,128)(2,1)S(1)} custom-call(bf16[512,2048]{1,0:T(8,128)(2,1)} %left.1, bf16[512,2048]{1,0:T(8,128)(2,1)} %right.1), custom_call_target="tpu_custom_call" | custom-call | tf_op jit(solution)/shard_map/pallas_call | solution.py:399
  97.7 1.3 %copy.4 = bf16[512,2048]{1,0:T(8,128)(2,1)} copy(bf16[512,2048]{1,0:T(8,128)(2,1)S(1)} %shard_map.28) | data formatting | bytes 4194304

commit v5 on v4

--- a/solution.py
+++ b/solution.py
@@ -17,7 +17,7 @@
 QUARTERS = 4
 NEAR = (0, 1, 2, 3)
 FAR = (7, 7, 7, 7)
-RELAY = (2, 3, 4, 5)
+RELAY = (1, 2, 3, 4)
 
 
 def remote(src, dst, sent, got, device):

time: 99.5 us -> 103 us (1.035)
  the two profiles are of different devices: /device:TPU:107 before, /device:TPU:118 now
where the time goes in v5:
time: 103 us
  Pallas kernels  102 us (99%)
  local copies, waits for them, and re-layouts  1.32 us (1%)
    pallas_call x1, Pallas kernels, local(): pl.pallas_call(kernel, out_shape=jax.ShapeDtypeStruct((size, width), jnp....  102 us

profile of v5, /device:TPU:118, one launch (start us, length us, event | category | flops | bytes accessed | tf_op | source)
XLA Modules:
  0.0 103.3 jit_solution(18355315592734609212)
XLA Ops:
  0.0 102.0 %shard_map.28 = bf16[512,2048]{1,0:T(8,128)(2,1)S(1)} custom-call(bf16[512,2048]{1,0:T(8,128)(2,1)} %left.1, bf16[512,2048]{1,0:T(8,128)(2,1)} %right.1), custom_call_target="tpu_custom_call" | custom-call | tf_op jit(solution)/shard_map/pallas_call | solution.py:399
  102.0 1.3 %copy.4 = bf16[512,2048]{1,0:T(8,128)(2,1)} copy(bf16[512,2048]{1,0:T(8,128)(2,1)S(1)} %shard_map.28) | data formatting | bytes 4194304
